TPU v7x, 32 devices: a whole 2x2x4 slice. The times are simulated.
32 devices in a mesh: dom: 8 (over y, x, core), col: 4 (over z).
Axes of the slice: x: 2, y: 2, z: 4, core: 2. Of those that a mesh axis runs over, the one named last changes fastest.
Arguments:
- features: bfloat16 [65536, 1024], P('dom', 'col')
- weight: bfloat16 [1024, 1024], P(None, 'col'), may hold values from -0.1875 to 0.1875
- out_bias: bfloat16 [1024], P('col'), may hold values from -3 to 3
- local_index: int32 [8, 64, 4], P('dom'), may hold values from 0 to 63
- local_count: int32 [8, 64], P('dom'), may hold values from 1 to 4, as said below
- local_vals: bfloat16 [8, 64, 4, 128, 128], P('dom'), may hold values from -0.1875 to 0.1875
- halo_index: int32 [8, 64, 4], P('dom'), may hold values from 0 to 31
- halo_count: int32 [8, 64], P('dom'), may hold values from 0 to 4, as said below
- halo_vals: bfloat16 [8, 64, 4, 128, 128], P('dom'), may hold values from -0.1875 to 0.1875
- send_rows: int32 [8, 8, 512], P('dom'), may hold values from 0 to 8191
- send_count: int32 [8, 8], P('dom'), may hold values from 0 to 512, as said below
Outputs:
- normalized: bfloat16 [65536, 1024], P('dom', 'col')
- channel_stats: float32 [2, 1024], P(None, 'col')
Inputs may be any that keep to these rules, and one draw needn't show every extreme that they name: `local_index`: slots k >= local_count of a row tile are not used. `local_count`: every partition has a row tile with all 4 slots used. `halo_index`: slots k >= halo_count of a row tile are not used. `halo_count`: every partition has a row tile with all 4 slots used. `send_rows`: slots s >= send_count[q, p] are not used. send_count[p, p] is 0; every partition fills all 512 slots to some other partition.
All inputs are finite; a program needn't handle non-finite values.
Results may differ from a plain program's by a relative error of at most 0.0075.
Values may be sent and summed in bfloat16 or wider, within the bound.
A program may use at most 192 MiB of HBM per device.

v0:
```python
import jax
import jax.numpy as jnp
from jax import lax
from jax.sharding import PartitionSpec as P

TILE = 128
epsilon = 1e-06


def tile_sum(sources, tile_index, tile_count, tile_vals):
    gathered = sources[tile_index]
    keep_mask = jnp.arange(tile_vals.shape[1])[None, :] < tile_count[:, None]
    masked = jnp.where(keep_mask[:, :, None, None], tile_vals, jnp.zeros_like(tile_vals))
    return jnp.einsum("tkij,tkjc->tic", masked, gathered, preferred_element_type=jnp.float32)


def on_device(
    features,
    weight,
    out_bias,
    local_index,
    local_count,
    local_vals,
    halo_index,
    halo_count,
    halo_vals,
    send_rows,
    send_count,
):
    row_count, col_width = features.shape
    peer_count = lax.axis_size("dom")
    slot_total = send_rows.shape[2]
    chosen = features[send_rows[0]]
    keep_mask = jnp.arange(slot_total)[None, :] < send_count[0][:, None]
    outgoing = jnp.where(keep_mask[:, :, None], chosen, jnp.zeros_like(chosen))
    arrived = lax.all_to_all(outgoing, "dom", split_axis=0, concat_axis=0, tiled=True)
    halo_tiles = arrived.reshape(peer_count * slot_total // TILE, TILE, col_width)
    own_tiles = features.reshape(row_count // TILE, TILE, col_width)
    summed = tile_sum(own_tiles, local_index[0], local_count[0], local_vals[0])
    summed = summed + tile_sum(halo_tiles, halo_index[0], halo_count[0], halo_vals[0])
    spread = summed.reshape(row_count, col_width).astype(jnp.bfloat16)
    node_total = row_count * peer_count
    regrouped = lax.all_to_all(spread, "col", split_axis=0, concat_axis=1, tiled=True)
    full_weight, full_bias = (
        lax.all_gather(weight, "col", axis=1, tiled=True),
        lax.all_gather(out_bias.reshape(1, col_width), "col", axis=1, tiled=True),
    )
    mixed_rows = jnp.dot(regrouped, full_weight, preferred_element_type=jnp.float32) + full_bias[
        0
    ].astype(jnp.float32)
    active = jnp.maximum(mixed_rows, 0.0)
    row_power = jnp.mean(active * active, axis=1, keepdims=True)
    scaled = active * lax.rsqrt(row_power + epsilon)
    sum_whole, square_whole = lax.psum(
        (jnp.sum(scaled, axis=0), jnp.sum(scaled * scaled, axis=0)), ("dom", "col")
    )
    normalized = lax.all_to_all(
        scaled.astype(jnp.bfloat16), "col", split_axis=1, concat_axis=0, tiled=True
    )
    column_start = lax.axis_index("col") * col_width
    sum_total = lax.dynamic_slice_in_dim(sum_whole, column_start, col_width, 0)
    square_total = lax.dynamic_slice_in_dim(square_whole, column_start, col_width, 0)
    channel_mean = sum_total / node_total
    channel_var = square_total / node_total - channel_mean * channel_mean
    return (normalized, jnp.stack([channel_mean, channel_var]))


def solution(mesh):
    in_specs = (
        P("dom", "col"),
        P(None, "col"),
        P("col"),
        P("dom", None, None),
        P("dom", None),
        P("dom", None, None, None, None),
        P("dom", None, None),
        P("dom", None),
        P("dom", None, None, None, None),
        P("dom", None, None),
        P("dom", None),
    )
    out_specs = (P("dom", "col"), P(None, "col"))
    return jax.shard_map(
        on_device, mesh=mesh, in_specs=in_specs, out_specs=out_specs, check_vma=False
    )
```

profile of v0, /device:TPU:0, one launch (start us, length us, event | category | flops | bytes accessed | tf_op | source)
XLA Modules:
  0.0 374.6 jit_solution(2426596609186330712)
XLA Ops:
  7.2 0.7 fusion.10
  7.9 0.7 iota_compare_fusion.2
  8.6 15.7 %gather_fusion.1 = bf16[4096,256]{1,0:T(8,128)(2,1)S(1)} fusion(bf16[8192,256]{1,0:T(8,128)(2,1)} %param.11, s32[4096]{0:T(1024)S(1)} %broadcast_clamp_fusion), kind=kCustom, calls=%fused_computation.1 | custom fusion | bytes 4210688 | tf_op jit(solution)/shard_map/gather | solution.py:33
  24.4 0.0 copy-start
  24.4 0.0 copy-start.1
  24.4 1.7 broadcast_select_fusion
  26.1 5.2 %all-to-all-start = ((bf16[8,512,256]{2,1,0:T(8,128)(2,1)}), bf16[8,512,256]{2,1,0:T(8,128)(2,1)S(1)}, u32[]{:S(2)}, u32[]{:S(2)}) async-start(bf16[8,512,256]{2,1,0:T(8,128)(2,1)} %broadcast_select_fusion), calls=%async_computation | async-start | bytes 4194304 | tf_op jit(solution)/shard_map/all_to_all | solution.py:36
  31.3 0.0 copy-done
  31.3 0.1 copy.19
  31.4 0.1 reshape.208
  31.5 0.0 copy-done.1
  31.5 0.1 copy.18
  31.6 0.1 reshape.192
  31.7 0.0 copy-start.2
  31.7 0.0 copy-start.3
  31.7 12.0 %gather_fusion = bf16[256,128,256]{2,1,0:T(8,128)(2,1)} fusion(bf16[64,128,256]{2,1,0:T(8,128)(2,1)} %bitcast.52, s32[1024]{0:T(1024)S(1)} %pad_clamp_fusion.1), kind=kCustom, calls=%fused_computation | custom fusion | bytes 33555456 | tf_op jit(solution)/shard_map/gather | solution.py:11
  43.7 0.0 copy-done.2
  43.7 0.1 iota_compare_fusion
  43.8 0.0 copy-done.3
  43.8 0.1 iota_compare_fusion.1
  43.9 14.0 %all-to-all-done = bf16[8,512,256]{2,1,0:T(8,128)(2,1)S(1)} async-done(((bf16[8,512,256]{2,1,0:T(8,128)(2,1)}), bf16[8,512,256]{2,1,0:T(8,128)(2,1)S(1)}, u32[]{:S(2)}, u32[]{:S(2)}) %all-to-all-start) | async-done | bytes 2097184 | tf_op jit(solution)/shard_map/all_to_all | solution.py:36
  57.9 9.7 %gather_fusion.2 = bf16[256,128,256]{2,1,0:T(8,128)(2,1)} fusion(bf16[32,128,256]{2,1,0:T(8,128)(2,1)S(1)} %bitcast.53, s32[1024]{0:T(1024)S(1)} %pad_clamp_fusion), kind=kCustom, calls=%fused_computation.2 | custom fusion | bytes 33555456 | tf_op jit(solution)/shard_map/gather | solution.py:11
  67.6 13.8 %fusion.1 = f32[64,128,256,1]{2,1,3,0:T(8,128)} fusion(bf16[64,4,128,256]{3,2,1,0:T(8,128)(2,1)} %bitcast.54, bf16[1,64,4,128,128]{4,3,2,1,0:T(8,128)(2,1)} %param.19, pred[64,4]{1,0:T(8,128)(4,1)S(1)} %iota_compare_fusion), kind=kOutput, calls=%fused_computation.6 | convolution fusion | flops 2151677952 | bytes 33554688 | tf_op jit(solution)/shard_map/tkij,tkjc->tic/dot_general | solution.py:14
  81.4 14.0 %fusion = bf16[64,128,256]{2,1,0:T(8,128)(2,1)} fusion(f32[64,128,256,1]{2,1,3,0:T(8,128)} %fusion.1, bf16[64,4,128,256]{3,2,1,0:T(8,128)(2,1)} %bitcast.55, bf16[1,64,4,128,128]{4,3,2,1,0:T(8,128)(2,1)} %param.16, pred[64,4]{1,0:T(8,128)(4,1)S(1)} %iota_compare_fusion.1), kind=kOutput, calls=%fused_computation.4 | convolution fusion | flops 2155872256 | bytes 37748992 | tf_op jit(solution)/shard_map/tkij,tkjc->tic/dot_general | solution.py:14
  95.4 0.0 copy-start.4
  95.4 6.3 %copy.20 = bf16[4,2048,256]{1,2,0:T(8,128)(2,1)} copy(bf16[4,2048,256]{2,1,0:T(8,128)(2,1)} %bitcast.56) | data formatting | bytes 8388608 | tf_op jit(solution)/shard_map/convert_element_type | solution.py:41
  101.6 4.9 %all-to-all-start.1 = ((bf16[4,2048,256]{1,2,0:T(8,128)(2,1)}), bf16[4,2048,256]{1,2,0:T(8,128)(2,1)}, u32[]{:S(2)}, u32[]{:S(2)}) async-start(bf16[4,2048,256]{1,2,0:T(8,128)(2,1)} %copy.20), calls=%async_computation.1 | async-start | bytes 8388608 | tf_op jit(solution)/shard_map/all_to_all | solution.py:43
  106.5 0.0 all-gather.4.cloned.1.call-start
  106.5 0.7 all-gather.4.cloned.1.call-update
  107.2 0.0 copy-done.4
  107.3 103.9 %all-gather.1 = bf16[4,1,256]{2,1,0:T(2,128)(2,1)S(1)} all-gather(bf16[1,1,256]{2,1,0:T(2,128)(2,1)S(1)} %reshape.220), channel_id=2, replica_groups=mesh['dom'=8,'col'=4] {'col'}, dimensions={0}, use_global_device_ids=true | all-gather | bytes 2560 | tf_op jit(solution)/shard_map/all_gather | solution.py:46
  211.2 0.0 all-gather.4.cloned.1.call-done
  211.2 19.8 %all-to-all-done.1 = bf16[4,2048,256]{1,2,0:T(8,128)(2,1)} async-done(((bf16[4,2048,256]{1,2,0:T(8,128)(2,1)}), bf16[4,2048,256]{1,2,0:T(8,128)(2,1)}, u32[]{:S(2)}, u32[]{:S(2)}) %all-to-all-start.1) | async-done | bytes 4194336 | tf_op jit(solution)/shard_map/all_to_all | solution.py:43
  231.0 7.8 %multiply_reduce_fusion.1 = (f32[2048]{0:T(1024)S(1)}, f32[2048,1024]{0,1:T(8,128)S(1)}) fusion(f32[1024]{0:T(1024)S(1)} %bitcast.61, bf16[2048,1024]{0,1:T(8,128)(2,1)} %bitcast.19, bf16[1024,1024]{1,0:T(8,128)(2,1)} %all-gather.4.cloned.1.call-done), kind=kOutput, calls=%fused_computation.10 | convolution fusion | flops 4303353856 | bytes 14692352 | tf_op jit(solution)/shard_map/dot_general | solution.py:48
  238.8 3.5 fusion.6
  242.2 4.8 %all-to-all-start.2 = ((bf16[2048,4,256]{0,2,1:T(8,128)(2,1)}), bf16[2048,4,256]{0,2,1:T(8,128)(2,1)}, u32[]{:S(2)}, u32[]{:S(2)}) async-start(bf16[2048,4,256]{0,2,1:T(8,128)(2,1)} %bitcast.57), calls=%async_computation.2 | async-start | bytes 8388608 | tf_op jit(solution)/shard_map/all_to_all | solution.py:57
  247.1 113.8 %all-reduce = (f32[1024]{0:T(1024)S(1)}, f32[1024]{0:T(1024)S(1)}) all-reduce(f32[1024]{0:T(1024)S(1)} %get-tuple-element.3, f32[1024]{0:T(1024)S(1)} %get-tuple-element.2), channel_id=1, replica_groups=mesh['dom'=8,'col'=4] {'dom','col'}, use_global_device_ids=true, to_apply=%region_4.5 | all-reduce | flops 2048 | bytes 16384 | tf_op jit(solution)/shard_map/psum | solution.py:54
  360.9 0.1 dynamic-slice_multiply_fusion
  361.0 0.6 pad_maximum_fusion
  361.5 0.0 all-to-all-done.2
  361.6 6.2 %copy.21 = bf16[4,2048,256]{2,1,0:T(8,128)(2,1)} copy(bf16[4,2048,256]{1,2,0:T(8,128)(2,1)} %bitcast.22) | data formatting | bytes 8388608 | tf_op jit(solution)/shard_map/all_to_all | solution.py:57
  (9 shorter events, 0.1 us)
Async XLA Ops:
  24.4 6.9 %copy-start = (s32[1,64,4]{1,2,0:T(4,128)S(1)}, s32[1,64,4]{1,2,0:T(4,128)}, u32[]{:S(2)}) copy-start(s32[1,64,4]{1,2,0:T(4,128)} %param.17) | copy-start | bytes 3076
  24.4 7.1 %copy-start.1 = (s32[1,64,4]{1,2,0:T(4,128)S(1)}, s32[1,64,4]{1,2,0:T(4,128)}, u32[]{:S(2)}) copy-start(s32[1,64,4]{1,2,0:T(4,128)} %param.14) | copy-start | bytes 3076
  26.1 31.8 %all-to-all-start = ((bf16[8,512,256]{2,1,0:T(8,128)(2,1)}), bf16[8,512,256]{2,1,0:T(8,128)(2,1)S(1)}, u32[]{:S(2)}, u32[]{:S(2)}) async-start(bf16[8,512,256]{2,1,0:T(8,128)(2,1)} %broadcast_select_fusion), calls=%async_computation | async-start | bytes 4194304 | tf_op jit(solution)/shard_map/all_to_all | solution.py:36
  31.7 12.0 %copy-start.2 = (s32[1,64]{1,0:T(1,128)S(1)}, s32[1,64]{1,0:T(1,128)}, u32[]{:S(2)}) copy-start(s32[1,64]{1,0:T(1,128)} %param.18) | copy-start | bytes 772
  31.7 12.1 %copy-start.3 = (s32[1,64]{1,0:T(1,128)S(1)}, s32[1,64]{1,0:T(1,128)}, u32[]{:S(2)}) copy-start(s32[1,64]{1,0:T(1,128)} %param.15) | copy-start | bytes 772
  95.4 11.9 %copy-start.4 = (bf16[256]{0:T(256)(128)(2,1)S(1)}, bf16[256]{0:T(256)(128)(2,1)}, u32[]{:S(2)}) copy-start(bf16[256]{0:T(256)(128)(2,1)} %param.13) | copy-start | bytes 1540
  101.6 129.3 %all-to-all-start.1 = ((bf16[4,2048,256]{1,2,0:T(8,128)(2,1)}), bf16[4,2048,256]{1,2,0:T(8,128)(2,1)}, u32[]{:S(2)}, u32[]{:S(2)}) async-start(bf16[4,2048,256]{1,2,0:T(8,128)(2,1)} %copy.20), calls=%async_computation.1 | async-start | bytes 8388608 | tf_op jit(solution)/shard_map/all_to_all | solution.py:43
  106.5 104.7 %all-gather.4.cloned.1.call-start = ((), (), s32[]{:S(2)}) async-start(), calls=%async_computation.3 | async-start | bytes 2621440 | tf_op jit(solution)/shard_map/all_gather | solution.py:45
  242.2 119.3 %all-to-all-start.2 = ((bf16[2048,4,256]{0,2,1:T(8,128)(2,1)}), bf16[2048,4,256]{0,2,1:T(8,128)(2,1)}, u32[]{:S(2)}, u32[]{:S(2)}) async-start(bf16[2048,4,256]{0,2,1:T(8,128)(2,1)} %bitcast.57), calls=%async_computation.2 | async-start | bytes 8388608 | tf_op jit(solution)/shard_map/all_to_all | solution.py:57
Sparse Core Ops, SparseCore 0:
  108.9 94.7 all-gather.3
where the time goes:
time: 375 us
  blocking collectives  218 us (58%)
  local copies, waits for them, and re-layouts  50.3 us (13%)
  matrix products  35.5 us (9%)
  waiting for transfers between devices  34.5 us (9%)
  starting transfers between devices  14.9 us (4%)
  between operations  14.2 us (4%)
  other arithmetic  7.48 us (2%)
    psum x1, blocking collectives, on_device(): lax.psum((jnp.sum(scaled, axis=0), jnp.sum(scaled * scaled, axis=0)), ('d...  114 us
    all_gather x1, blocking collectives, on_device(): lax.all_gather(out_bias.reshape(1, col_width), 'col', axis=1, tiled=True)  104 us
    dot_general x2, matrix products, tile_sum(): jnp.einsum('tkij,tkjc->tic', masked, gathered, preferred_element_type=jnp...  27.7 us
    gather x2, local copies, waits for them, and re-layouts, tile_sum(): gathered = sources[tile_index]  21.7 us
    all_to_all x1, waiting for transfers between devices, on_device(): lax.all_to_all(spread, 'col', split_axis=0, concat_axis=1, tiled=True)  19.8 us
    gather x1, local copies, waits for them, and re-layouts, on_device(): chosen = features[send_rows[0]]  15.7 us
    all_to_all x1, waiting for transfers between devices, on_device(): lax.all_to_all(outgoing, 'dom', split_axis=0, concat_axis=0, tiled=True)  14 us
    dot_general x1, matrix products, on_device(): jnp.dot(regrouped, full_weight, preferred_element_type=jnp.float32)  7.76 us
  transfers between devices with their start and end apart: 4, of which 2 were waited for; matrix products, arithmetic and copies ran while one was open for 4% of the time, Pallas kernels for 0%

commit v1 on v0

--- a/solution.py
+++ b/solution.py
@@ -5,6 +5,18 @@
 
 TILE = 128
 epsilon = 1e-06
+
+
+def gather_by_bits(array, axis, dim):
+    ways, here, hop = (lax.axis_size(axis), lax.axis_index(axis), array.shape[dim])
+    line, have = (array, 1)
+    while have < ways:
+        line = jnp.concatenate(
+            [line, lax.ppermute(line, axis, [(d, (d - have) % ways) for d in range(ways)])],
+            axis=dim,
+        )
+        have = 2 * have
+    return jnp.roll(line, here * hop, axis=dim)
 
 
 def tile_sum(sources, tile_index, tile_count, tile_vals):
@@ -43,7 +55,7 @@
     regrouped = lax.all_to_all(spread, "col", split_axis=0, concat_axis=1, tiled=True)
     full_weight, full_bias = (
         lax.all_gather(weight, "col", axis=1, tiled=True),
-        lax.all_gather(out_bias.reshape(1, col_width), "col", axis=1, tiled=True),
+        gather_by_bits(out_bias.reshape(1, col_width), "col", 1),
     )
     mixed_rows = jnp.dot(regrouped, full_weight, preferred_element_type=jnp.float32) + full_bias[
         0

time: 375 us -> 377 us (level)
  blocking collectives: 218 us -> 114 us
  waiting for transfers between devices: 34.5 us -> 110 us
  starting transfers between devices: 14.9 us -> 44.3 us
    all_gather x1 -> x0, blocking collectives: 104 us -> none  [on_device(): lax.all_gather(out_bias.reshape(1, col_width), 'col', axis=1, tiled=True)]
    ppermute x0 -> x2, waiting for transfers between devices: none -> 95.7 us  [gather_by_bits(): lax.ppermute(line, axis, [(d, (d - have) % ways) for d in range(ways)])]
    ppermute x0 -> x2, starting transfers between devices: none -> 29.1 us  [gather_by_bits(): lax.ppermute(line, axis, [(d, (d - have) % ways) for d in range(ways)])]
    all_to_all x1, waiting for transfers between devices: 19.8 us -> 0.01 us  [on_device(): lax.all_to_all(spread, 'col', split_axis=0, concat_axis=1, tiled=True)]
  transfers between devices with their start and end apart: 4 -> 6, of which waited for: 2 -> 3; matrix products, arithmetic and copies ran while one was open for 4% -> 4% of each run, Pallas kernels for 0% -> 0%
where the time goes in v1:
time: 377 us; the launch traced here: 376 us
  blocking collectives  114 us (30%)
  waiting for transfers between devices  110 us (29%)
  local copies, waits for them, and re-layouts  50.4 us (13%)
  starting transfers between devices  44.3 us (12%)
  matrix products  35.5 us (9%)
  between operations  14.2 us (4%)
  other arithmetic  7.49 us (2%)
    psum x1, blocking collectives, on_device(): lax.psum((jnp.sum(scaled, axis=0), jnp.sum(scaled * scaled, axis=0)), ('d...  114 us
    ppermute x2, waiting for transfers between devices, gather_by_bits(): lax.ppermute(line, axis, [(d, (d - have) % ways) for d in range(ways)])  95.7 us
    ppermute x2, starting transfers between devices, gather_by_bits(): lax.ppermute(line, axis, [(d, (d - have) % ways) for d in range(ways)])  29.1 us
    dot_general x2, matrix products, tile_sum(): jnp.einsum('tkij,tkjc->tic', masked, gathered, preferred_element_type=jnp...  27.7 us
    gather x2, local copies, waits for them, and re-layouts, tile_sum(): gathered = sources[tile_index]  21.7 us
    gather x1, local copies, waits for them, and re-layouts, on_device(): chosen = features[send_rows[0]]  15.7 us
    all_to_all x1, waiting for transfers between devices, on_device(): lax.all_to_all(outgoing, 'dom', split_axis=0, concat_axis=0, tiled=True)  14 us
    dot_general x1, matrix products, on_device(): jnp.dot(regrouped, full_weight, preferred_element_type=jnp.float32)  7.77 us
  transfers between devices with their start and end apart: 6, of which 3 were waited for; matrix products, arithmetic and copies ran while one was open for 4% of the time, Pallas kernels for 0%

profile of v1, /device:TPU:0, one launch (start us, length us, event | category | flops | bytes accessed | tf_op | source)
XLA Modules:
  0.0 376.4 jit_solution(2648290293444759671)
XLA Ops:
  7.2 0.7 fusion.10
  7.9 0.7 iota_compare_fusion.2
  8.6 15.7 %gather_fusion.1 = bf16[4096,256]{1,0:T(8,128)(2,1)S(1)} fusion(bf16[8192,256]{1,0:T(8,128)(2,1)} %param.11, s32[4096]{0:T(1024)S(1)} %broadcast_clamp_fusion), kind=kCustom, calls=%fused_computation.1 | custom fusion | bytes 4210688 | tf_op jit(solution)/shard_map/gather | solution.py:45
  24.4 0.0 copy-start
  24.4 0.0 copy-start.1
  24.4 1.7 broadcast_select_fusion
  26.1 5.2 %all-to-all-start = ((bf16[8,512,256]{2,1,0:T(8,128)(2,1)}), bf16[8,512,256]{2,1,0:T(8,128)(2,1)S(1)}, u32[]{:S(2)}, u32[]{:S(2)}) async-start(bf16[8,512,256]{2,1,0:T(8,128)(2,1)} %broadcast_select_fusion), calls=%async_computation | async-start | bytes 4194304 | tf_op jit(solution)/shard_map/all_to_all | solution.py:48
  31.3 0.0 copy-done
  31.3 0.1 copy.15
  31.4 0.1 reshape.208
  31.5 0.0 copy-done.1
  31.5 0.1 copy.14
  31.6 0.1 reshape.192
  31.7 0.0 copy-start.2
  31.7 0.0 copy-start.3
  31.7 12.0 %gather_fusion = bf16[256,128,256]{2,1,0:T(8,128)(2,1)} fusion(bf16[64,128,256]{2,1,0:T(8,128)(2,1)} %bitcast.52, s32[1024]{0:T(1024)S(1)} %pad_clamp_fusion.1), kind=kCustom, calls=%fused_computation | custom fusion | bytes 33555456 | tf_op jit(solution)/shard_map/gather | solution.py:23
  43.7 0.0 copy-done.2
  43.7 0.1 iota_compare_fusion
  43.8 0.0 copy-done.3
  43.8 0.1 iota_compare_fusion.1
  43.9 14.0 %all-to-all-done = bf16[8,512,256]{2,1,0:T(8,128)(2,1)S(1)} async-done(((bf16[8,512,256]{2,1,0:T(8,128)(2,1)}), bf16[8,512,256]{2,1,0:T(8,128)(2,1)S(1)}, u32[]{:S(2)}, u32[]{:S(2)}) %all-to-all-start) | async-done | bytes 2097184 | tf_op jit(solution)/shard_map/all_to_all | solution.py:48
  57.9 9.7 %gather_fusion.2 = bf16[256,128,256]{2,1,0:T(8,128)(2,1)} fusion(bf16[32,128,256]{2,1,0:T(8,128)(2,1)S(1)} %bitcast.53, s32[1024]{0:T(1024)S(1)} %pad_clamp_fusion), kind=kCustom, calls=%fused_computation.2 | custom fusion | bytes 33555456 | tf_op jit(solution)/shard_map/gather | solution.py:23
  67.6 13.8 %fusion.1 = f32[64,128,256,1]{2,1,3,0:T(8,128)} fusion(bf16[64,4,128,256]{3,2,1,0:T(8,128)(2,1)} %bitcast.54, bf16[1,64,4,128,128]{4,3,2,1,0:T(8,128)(2,1)} %param.19, pred[64,4]{1,0:T(8,128)(4,1)S(1)} %iota_compare_fusion), kind=kOutput, calls=%fused_computation.6 | convolution fusion | flops 2151677952 | bytes 33554688 | tf_op jit(solution)/shard_map/tkij,tkjc->tic/dot_general | solution.py:26
  81.4 14.0 %fusion = bf16[64,128,256]{2,1,0:T(8,128)(2,1)} fusion(f32[64,128,256,1]{2,1,3,0:T(8,128)} %fusion.1, bf16[64,4,128,256]{3,2,1,0:T(8,128)(2,1)} %bitcast.55, bf16[1,64,4,128,128]{4,3,2,1,0:T(8,128)(2,1)} %param.16, pred[64,4]{1,0:T(8,128)(4,1)S(1)} %iota_compare_fusion.1), kind=kOutput, calls=%fused_computation.4 | convolution fusion | flops 2155872256 | bytes 37748992 | tf_op jit(solution)/shard_map/tkij,tkjc->tic/dot_general | solution.py:26
  95.4 0.0 copy-start.4
  95.4 6.3 %copy.16 = bf16[4,2048,256]{1,2,0:T(8,128)(2,1)} copy(bf16[4,2048,256]{2,1,0:T(8,128)(2,1)} %bitcast.56) | data formatting | bytes 8388608 | tf_op jit(solution)/shard_map/convert_element_type | solution.py:53
  101.6 4.9 %all-to-all-start.1 = ((bf16[4,2048,256]{1,2,0:T(8,128)(2,1)}), bf16[4,2048,256]{1,2,0:T(8,128)(2,1)}, u32[]{:S(2)}, u32[]{:S(2)}) async-start(bf16[4,2048,256]{1,2,0:T(8,128)(2,1)} %copy.16), calls=%async_computation.1 | async-start | bytes 8388608 | tf_op jit(solution)/shard_map/all_to_all | solution.py:55
  106.5 0.0 all-gather.2.cloned.1.call-start
  106.5 0.7 all-gather.2.cloned.1.call-update
  107.2 0.0 copy-done.4
  107.2 4.1 %collective-permute-start = (bf16[1,256]{1,0:T(2,128)(2,1)S(1)}, bf16[1,256]{1,0:T(2,128)(2,1)S(1)}, u32[]{:S(2)}, u32[]{:S(2)}) collective-permute-start(bf16[1,256]{1,0:T(2,128)(2,1)S(1)} %reshape.188), channel_id=1, source_target_pairs={{0,3},{1,0},{2,1},{3,2},{4,7},{5,4},{6,5},{7,6},{8,11},{9,8},{10,9... | collective-permute-start | bytes 1544 | tf_op jit(solution)/shard_map/ppermute | solution.py:15
  111.3 94.1 %collective-permute-done = bf16[1,256]{1,0:T(2,128)(2,1)S(1)} collective-permute-done((bf16[1,256]{1,0:T(2,128)(2,1)S(1)}, bf16[1,256]{1,0:T(2,128)(2,1)S(1)}, u32[]{:S(2)}, u32[]{:S(2)}) %collective-permute-start) | collective-permute-done | bytes 544 | tf_op jit(solution)/shard_map/ppermute | solution.py:15
  205.4 25.1 %collective-permute-start.1 = (bf16[1,512]{1,0:T(2,128)(2,1)S(1)}, bf16[1,512]{1,0:T(2,128)(2,1)S(1)}, u32[]{:S(2)}, u32[]{:S(2)}) collective-permute-start(bf16[1,512]{1,0:T(2,128)(2,1)S(1)} %pad_maximum_fusion), channel_id=1, source_target_pairs={{0,2},{1,3},{2,0},{3,1},{4,6},{5,7},{6,4},{7,5},{8,10},{9,11},{10,... | collective-permute-start | bytes 3080 | tf_op jit(solution)/shard_map/ppermute | solution.py:15
  230.5 1.6 collective-permute-done.1
  232.1 0.0 all-gather.2.cloned.1.call-done
  232.1 0.0 all-to-all-done.1
  232.1 7.8 %multiply_reduce_fusion.1 = (f32[2048]{0:T(1024)S(1)}, f32[2048,1024]{0,1:T(8,128)S(1)}) fusion(f32[1024]{0:T(1024)S(1)} %bitcast.61, bf16[2048,1024]{0,1:T(8,128)(2,1)} %bitcast.19, bf16[1024,1024]{1,0:T(8,128)(2,1)} %all-gather.2.cloned.1.call-done), kind=kOutput, calls=%fused_computation.10 | convolution fusion | flops 4303353856 | bytes 14692352 | tf_op jit(solution)/shard_map/dot_general | solution.py:60
  239.9 3.5 fusion.6
  243.4 5.1 %all-to-all-start.2 = ((bf16[2048,4,256]{0,2,1:T(8,128)(2,1)}), bf16[2048,4,256]{0,2,1:T(8,128)(2,1)}, u32[]{:S(2)}, u32[]{:S(2)}) async-start(bf16[2048,4,256]{0,2,1:T(8,128)(2,1)} %bitcast.57), calls=%async_computation.2 | async-start | bytes 8388608 | tf_op jit(solution)/shard_map/all_to_all | solution.py:69
  248.5 114.2 %all-reduce = (f32[1024]{0:T(1024)S(1)}, f32[1024]{0:T(1024)S(1)}) all-reduce(f32[1024]{0:T(1024)S(1)} %get-tuple-element.3, f32[1024]{0:T(1024)S(1)} %get-tuple-element.2), channel_id=1, replica_groups=mesh['dom'=8,'col'=4] {'dom','col'}, use_global_device_ids=true, to_apply=%region_4.5 | all-reduce | flops 2048 | bytes 16384 | tf_op jit(solution)/shard_map/psum | solution.py:66
  362.7 0.1 dynamic-slice_multiply_fusion
  362.8 0.6 pad_maximum_fusion.1
  363.4 0.0 all-to-all-done.2
  363.4 6.2 %copy.17 = bf16[4,2048,256]{2,1,0:T(8,128)(2,1)} copy(bf16[4,2048,256]{1,2,0:T(8,128)(2,1)} %bitcast.22) | data formatting | bytes 8388608 | tf_op jit(solution)/shard_map/all_to_all | solution.py:69
  (16 shorter events, 0.1 us)
Async XLA Ops:
  24.4 6.9 %copy-start = (s32[1,64,4]{1,2,0:T(4,128)S(1)}, s32[1,64,4]{1,2,0:T(4,128)}, u32[]{:S(2)}) copy-start(s32[1,64,4]{1,2,0:T(4,128)} %param.17) | copy-start | bytes 3076
  24.4 7.1 %copy-start.1 = (s32[1,64,4]{1,2,0:T(4,128)S(1)}, s32[1,64,4]{1,2,0:T(4,128)}, u32[]{:S(2)}) copy-start(s32[1,64,4]{1,2,0:T(4,128)} %param.14) | copy-start | bytes 3076
  26.1 31.8 %all-to-all-start = ((bf16[8,512,256]{2,1,0:T(8,128)(2,1)}), bf16[8,512,256]{2,1,0:T(8,128)(2,1)S(1)}, u32[]{:S(2)}, u32[]{:S(2)}) async-start(bf16[8,512,256]{2,1,0:T(8,128)(2,1)} %broadcast_select_fusion), calls=%async_computation | async-start | bytes 4194304 | tf_op jit(solution)/shard_map/all_to_all | solution.py:48
  31.7 12.0 %copy-start.2 = (s32[1,64]{1,0:T(1,128)S(1)}, s32[1,64]{1,0:T(1,128)}, u32[]{:S(2)}) copy-start(s32[1,64]{1,0:T(1,128)} %param.18) | copy-start | bytes 772
  31.7 12.1 %copy-start.3 = (s32[1,64]{1,0:T(1,128)S(1)}, s32[1,64]{1,0:T(1,128)}, u32[]{:S(2)}) copy-start(s32[1,64]{1,0:T(1,128)} %param.15) | copy-start | bytes 772
  95.4 11.9 %copy-start.4 = (bf16[256]{0:T(256)(128)(2,1)S(1)}, bf16[256]{0:T(256)(128)(2,1)}, u32[]{:S(2)}) copy-start(bf16[256]{0:T(256)(128)(2,1)} %param.13) | copy-start | bytes 1540
  101.6 130.5 %all-to-all-start.1 = ((bf16[4,2048,256]{1,2,0:T(8,128)(2,1)}), bf16[4,2048,256]{1,2,0:T(8,128)(2,1)}, u32[]{:S(2)}, u32[]{:S(2)}) async-start(bf16[4,2048,256]{1,2,0:T(8,128)(2,1)} %copy.16), calls=%async_computation.1 | async-start | bytes 8388608 | tf_op jit(solution)/shard_map/all_to_all | solution.py:55
  106.5 125.6 %all-gather.2.cloned.1.call-start = ((), (), s32[]{:S(2)}) async-start(), calls=%async_computation.3 | async-start | bytes 2621440 | tf_op jit(solution)/shard_map/all_gather | solution.py:57
  107.2 98.2 %collective-permute-start = (bf16[1,256]{1,0:T(2,128)(2,1)S(1)}, bf16[1,256]{1,0:T(2,128)(2,1)S(1)}, u32[]{:S(2)}, u32[]{:S(2)}) collective-permute-start(bf16[1,256]{1,0:T(2,128)(2,1)S(1)} %reshape.188), channel_id=1, source_target_pairs={{0,3},{1,0},{2,1},{3,2},{4,7},{5,4},{6,5},{7,6},{8,11},{9,8},{10,9... | collective-permute-start | bytes 1544 | tf_op jit(solution)/shard_map/ppermute | solution.py:15
  205.4 26.6 %collective-permute-start.1 = (bf16[1,512]{1,0:T(2,128)(2,1)S(1)}, bf16[1,512]{1,0:T(2,128)(2,1)S(1)}, u32[]{:S(2)}, u32[]{:S(2)}) collective-permute-start(bf16[1,512]{1,0:T(2,128)(2,1)S(1)} %pad_maximum_fusion), channel_id=1, source_target_pairs={{0,2},{1,3},{2,0},{3,1},{4,6},{5,7},{6,4},{7,5},{8,10},{9,11},{10,... | collective-permute-start | bytes 3080 | tf_op jit(solution)/shard_map/ppermute | solution.py:15
  243.4 120.0 %all-to-all-start.2 = ((bf16[2048,4,256]{0,2,1:T(8,128)(2,1)}), bf16[2048,4,256]{0,2,1:T(8,128)(2,1)}, u32[]{:S(2)}, u32[]{:S(2)}) async-start(bf16[2048,4,256]{0,2,1:T(8,128)(2,1)} %bitcast.57), calls=%async_computation.2 | async-start | bytes 8388608 | tf_op jit(solution)/shard_map/all_to_all | solution.py:69
Sparse Core Ops, SparseCore 0:
  108.9 94.7 all-gather.1
